TPU v7x, 32 devices: a whole 2x2x4 slice. The times are simulated.
32 devices in a mesh: dp: 8 (over y, x, core), seq: 4 (over z).
Axes of the slice: x: 2, y: 2, z: 4, core: 2. Of those that a mesh axis runs over, the one named last changes fastest.
Arguments:
- tokens_in: bfloat16 [16, 1024, 1536], P('dp', 'seq'), may hold values from -6 to 6
- expert_ids: int32 [16, 1024, 8], P('dp', 'seq'), may hold values from 0 to 15, all different within a row; in each aligned block of 256 rows (0 to 255, 256 to 511, ..., all dimensions but the last counted through in order) at most 160 rows name the same one
- prefix_len: int32 [16], P('dp'), may hold values from 102 to 512
- attn_gain: float32 [1536], P(('dp', 'seq')), may hold values from 0.25 to 1.75
- w_qkv: float32 [1536, 2560], P(('dp', 'seq')), may hold values from -0.625 to 0.625
- w_out: float32 [1536, 1536], P(None, ('dp', 'seq')), may hold values from -0.875 to 0.875
- ffn_gain: float32 [1536], P(('dp', 'seq')), may hold values from 0.25 to 1.75
- w_router: float32 [1536, 16], P(('dp', 'seq')), may hold values from -0.078125 to 0.078125
- w_gate_up: float32 [16, 1536, 1024], P('seq', 'dp'), may hold values from -0.3125 to 0.3125
- w_down: float32 [16, 512, 1536], P('seq', None, 'dp'), may hold values from -1 to 1
- out_grad: bfloat16 [16, 1024, 1536], P('dp', 'seq'), may hold values from -6 to 6
Outputs:
- activations: bfloat16 [16, 1024, 1536], P('dp', 'seq')
- input_grad: float32 [16, 1024, 1536], P('dp', 'seq')
- grad_attn_gain: float32 [1536], P(('dp', 'seq'))
- grad_w_qkv: float32 [1536, 2560], P(('dp', 'seq'))
- grad_w_out: float32 [1536, 1536], P(None, ('dp', 'seq'))
- grad_ffn_gain: float32 [1536], P(('dp', 'seq'))
- grad_w_router: float32 [1536, 16], P(('dp', 'seq'))
- grad_w_gate_up: float32 [16, 1536, 1024], P('seq', 'dp')
- grad_w_down: float32 [16, 512, 1536], P('seq', None, 'dp')
Inputs may be any that keep to these rules, and one draw needn't show every extreme that they name: `expert_ids`: within the 256 rows of one sequence on one device (aligned blocks of rows), no expert is named by more than 160 rows, and some block in every draw has an expert named by exactly 160 rows; the 8 experts of a token differ.
All inputs are finite; a program needn't handle non-finite values.
Results may differ from a plain program's by a relative error of at most 0.02.
The roundings to bfloat16 on the way count: a program that leaves them out, or rounds other values in their place, can miss the bound.
Values may be sent and summed in bfloat16 or wider, within the bound.
A program may use at most 448 MiB of HBM per device.

v0:
```python
import jax
import jax.numpy as jnp
from jax import lax
from jax.sharding import PartitionSpec as P

HEADS = 24
KV = 8
HD = 64
EXPERTS = 16


EPSILON = 1e-06
SCORE_SCALE = 0.015625
RESIDUAL_FACTOR = 0.22
ROTARY_BASE = 10000.0
NEGATIVE_FILL = -1e30


def rotary_tables(positions):
    half_size = HD // 2
    inverse = ROTARY_BASE ** (-(jnp.arange(half_size, dtype=jnp.float32) * 2.0 / HD))
    angles = positions.astype(jnp.float32)[:, None] * inverse[None, :]
    return (jnp.cos(angles)[:, None, :], jnp.sin(angles)[:, None, :])


def rotate(values, cosine_table, sine_table, direction):
    half_size = values.shape[-1] // 2
    first_half = values[..., :half_size]
    second_half = values[..., half_size:]
    return jnp.concatenate(
        [
            first_half * cosine_table - direction * second_half * sine_table,
            second_half * cosine_table + direction * first_half * sine_table,
        ],
        axis=-1,
    )


def expert_slots(routed, capacity):
    one_hot = (routed[..., None] == jnp.arange(EXPERTS, dtype=jnp.int32)).astype(jnp.int32)
    before = jnp.cumsum(one_hot, axis=1) - one_hot
    return routed * capacity + jnp.sum(before * one_hot, axis=-1)


def masked_scores(queries, key_block, query_pos, key_pos, prefixes):
    seq_count, key_count = (key_block.shape[0], key_block.shape[1])
    keys_four = key_block.reshape(seq_count, key_count, KV, HD)
    scores = (
        jnp.einsum("sqhgd,skhd->shgqk", queries, keys_four, preferred_element_type=jnp.float32)
        * SCORE_SCALE
    )
    allowed = (key_pos[None, None, :] <= query_pos[None, :, None]) | (
        key_pos[None, None, :] < prefixes[:, None, None]
    ) & (query_pos[None, :, None] < prefixes[:, None, None])
    return (jnp.where(allowed[:, None, None], scores, NEGATIVE_FILL), keys_four)


def place_rows(source, slot_row, slot_total):
    return jnp.zeros((slot_total, source.shape[-1]), source.dtype).at[slot_row].set(source)


def take_rows(source, slot_row):
    return source[slot_row]


def norm_back(grad_norm, attention_input_normed, scale_row):
    return scale_row * (
        grad_norm
        - attention_input_normed
        * jnp.mean(grad_norm * attention_input_normed, axis=-1, keepdims=True)
    )


def fetch_weights(attn_gain, w_qkv, w_out, ffn_gain, w_router, w_gate_up, w_down):
    small_set = (
        lax.all_gather(attn_gain.astype(jnp.bfloat16), ("dp", "seq"), axis=0, tiled=True),
        lax.all_gather(w_qkv.astype(jnp.bfloat16), ("dp", "seq"), axis=0, tiled=True),
        lax.all_gather(w_out.astype(jnp.bfloat16), ("dp", "seq"), axis=1, tiled=True),
        lax.all_gather(ffn_gain.astype(jnp.bfloat16), ("dp", "seq"), axis=0, tiled=True),
        lax.all_gather(w_router.astype(jnp.bfloat16), ("dp", "seq"), axis=0, tiled=True),
    )
    gate_up_weight, down_weight = (
        lax.all_gather(w_gate_up.astype(jnp.bfloat16), "dp", axis=1, tiled=True),
        lax.all_gather(w_down.astype(jnp.bfloat16), "dp", axis=2, tiled=True),
    )
    return tuple(small_set) + (gate_up_weight, down_weight)


def expert_forward(rows, gate_up_weight, down_weight):
    hidden = down_weight.shape[1]
    gate_up = jnp.einsum("secd,edf->secf", rows, gate_up_weight, preferred_element_type=jnp.float32)
    gate_part = gate_up[..., :hidden]
    up_part = gate_up[..., hidden:]
    sigmoid_gate = jax.nn.sigmoid(gate_part)
    activated = (gate_part * sigmoid_gate * up_part).astype(jnp.bfloat16)
    expert_out = jnp.einsum(
        "secf,efd->secd", activated, down_weight, preferred_element_type=jnp.float32
    ).astype(jnp.bfloat16)
    return (gate_part, up_part, sigmoid_gate, activated, expert_out)


def expert_backward(grad_rows, gate_part, up_part, sigmoid_gate, gate_up_weight, down_weight):
    grad_act = jnp.einsum(
        "secd,efd->secf", grad_rows, down_weight, preferred_element_type=jnp.float32
    )
    grad_gate = grad_act * up_part * (sigmoid_gate * (1.0 + gate_part * (1.0 - sigmoid_gate)))
    grad_up = grad_act * gate_part * sigmoid_gate
    grad_gate_up = jnp.concatenate([grad_gate, grad_up], axis=-1).astype(jnp.bfloat16)
    grad_inputs = jnp.einsum(
        "secf,edf->secd", grad_gate_up, gate_up_weight, preferred_element_type=jnp.float32
    )
    return (grad_gate_up, grad_inputs)


def body(
    tokens_in,
    expert_ids,
    prefix_len,
    attn_gain,
    w_qkv,
    w_out,
    ffn_gain,
    w_router,
    w_gate_up,
    w_down,
    out_grad,
):
    seq_count, seg_len, model_width = tokens_in.shape
    route_count = expert_ids.shape[2]
    query_group = HEADS // KV
    capacity = max(2, seg_len * route_count * 5 // (4 * EXPERTS))
    slot_total = EXPERTS * capacity
    masters = (attn_gain, w_qkv, w_out, ffn_gain, w_router, w_gate_up, w_down)
    forward_set = fetch_weights(*masters)
    (
        gain_attn,
        query_key_value_matrix,
        output_matrix,
        gain_ffn,
        routing_matrix,
        gate_up_weight,
        down_weight,
    ) = forward_set
    inputs = tokens_in.astype(jnp.float32)
    scale_one = lax.rsqrt(jnp.mean(inputs * inputs, axis=-1, keepdims=True) + EPSILON)
    normed_one = inputs * scale_one
    attention_input_normed = (normed_one * gain_attn.astype(jnp.float32)).astype(jnp.bfloat16)
    output_projection = jnp.einsum(
        "rcp,pa->rca",
        attention_input_normed,
        query_key_value_matrix,
        preferred_element_type=jnp.float32,
    )
    query_pos = lax.axis_index("seq") * seg_len + jnp.arange(seg_len, dtype=jnp.int32)
    cosine_table, sine_table = rotary_tables(query_pos)
    queries = rotate(
        output_projection[..., : HEADS * HD].reshape(seq_count, seg_len, HEADS, HD),
        cosine_table,
        sine_table,
        1.0,
    )
    queries = queries.astype(jnp.bfloat16).reshape(seq_count, seg_len, KV, query_group, HD)
    keys_local = rotate(
        output_projection[..., HEADS * HD : (HEADS + KV) * HD].reshape(seq_count, seg_len, KV, HD),
        cosine_table,
        sine_table,
        1.0,
    )
    keys_local = keys_local.astype(jnp.bfloat16).reshape(seq_count, seg_len, KV * HD)
    values_local = output_projection[..., (HEADS + KV) * HD :].astype(jnp.bfloat16)
    start_state = (
        jnp.full((seq_count, KV, query_group, seg_len), NEGATIVE_FILL, jnp.float32),
        jnp.zeros((seq_count, KV, query_group, seg_len), jnp.float32),
        jnp.zeros((seq_count, KV, query_group, seg_len, HD), jnp.float32),
    )
    key_piece = lax.all_gather(keys_local, "seq", axis=1, tiled=True)
    value_piece = lax.all_gather(values_local, "seq", axis=1, tiled=True)
    piece_len = key_piece.shape[1]
    block_len = 512

    def one_block(run_state, block_number):
        run_max, run_sum, run_acc = run_state
        offset = block_number * block_len
        key_block = lax.dynamic_slice_in_dim(key_piece, offset, block_len, 1)
        value_block = lax.dynamic_slice_in_dim(value_piece, offset, block_len, 1)
        key_pos = offset + jnp.arange(block_len, dtype=jnp.int32)
        scores, keys_four = masked_scores(queries, key_block, query_pos, key_pos, prefix_len)
        new_max = jnp.maximum(run_max, jnp.max(scores, axis=-1))
        fading = jnp.exp(run_max - new_max)
        exp_weights = jnp.exp(scores - new_max[..., None])
        run_sum = run_sum * fading + jnp.sum(exp_weights, axis=-1)
        values_four = value_block.reshape(seq_count, block_len, KV, HD)
        addition = jnp.einsum(
            "shgqk,skhd->shgqd",
            exp_weights.astype(jnp.bfloat16),
            values_four,
            preferred_element_type=jnp.float32,
        )
        return ((new_max, run_sum, run_acc * fading[..., None] + addition), None)

    carry_out, ignored = lax.scan(
        one_block, start_state, jnp.arange(piece_len // block_len, dtype=jnp.int32)
    )
    row_max, sum_exp, unnorm = carry_out
    sum_rows = jnp.transpose(sum_exp, (0, 3, 1, 2))
    attended_full = jnp.transpose(unnorm, (0, 3, 1, 2, 4)) / sum_rows[..., None]
    attention_result = attended_full.reshape(seq_count, seg_len, HEADS * HD).astype(jnp.bfloat16)
    initial_residual_sum = inputs + RESIDUAL_FACTOR * jnp.einsum(
        "rtm,mg->rtg", attention_result, output_matrix, preferred_element_type=jnp.float32
    )
    scale_two = lax.rsqrt(
        jnp.mean(initial_residual_sum * initial_residual_sum, axis=-1, keepdims=True) + EPSILON
    )
    normed_two = initial_residual_sum * scale_two
    feedforward_input_normed = (normed_two * gain_ffn.astype(jnp.float32)).astype(jnp.bfloat16)
    router_scores = jnp.einsum(
        "rcp,pa->rca", feedforward_input_normed, routing_matrix, preferred_element_type=jnp.float32
    )
    one_hot = (expert_ids[..., None] == jnp.arange(EXPERTS, dtype=jnp.int32)).astype(jnp.float32)
    chosen = jnp.sum(one_hot * router_scores[:, :, None, :], axis=-1)
    gate_weights = jax.nn.softmax(chosen, axis=-1)
    slot_index = expert_slots(expert_ids.reshape(seq_count, seg_len * route_count), capacity)
    repeated = jnp.repeat(feedforward_input_normed, route_count, axis=1)
    buffers = jax.vmap(place_rows, in_axes=(0, 0, None))(repeated, slot_index, slot_total)
    buffers = buffers.reshape(seq_count, EXPERTS, capacity, model_width)
    expert_rows = lax.all_to_all(buffers, "seq", split_axis=1, concat_axis=0, tiled=True)
    gate_part, up_part, sigmoid_gate, activated, owner_out = expert_forward(
        expert_rows, gate_up_weight, down_weight
    )
    expert_out = lax.all_to_all(owner_out, "seq", split_axis=0, concat_axis=1, tiled=True)
    picked = jax.vmap(take_rows)(expert_out.reshape(seq_count, slot_total, model_width), slot_index)
    picked = picked.reshape(seq_count, seg_len, route_count, model_width)
    result = initial_residual_sum + RESIDUAL_FACTOR * jnp.sum(
        gate_weights[..., None] * picked, axis=2
    )
    activations = result.astype(jnp.bfloat16)
    backward_set = fetch_weights(*masters)
    (
        gain_attn,
        query_key_value_matrix,
        output_matrix,
        gain_ffn,
        routing_matrix,
        gate_up_weight,
        down_weight,
    ) = backward_set
    grad_output = out_grad.astype(jnp.float32)
    grad_mixed = RESIDUAL_FACTOR * grad_output
    grad_gates = jnp.sum(grad_mixed[:, :, None, :] * picked, axis=-1)
    grad_chosen = gate_weights * (
        grad_gates - jnp.sum(gate_weights * grad_gates, axis=-1, keepdims=True)
    )
    grad_picked = (gate_weights[..., None] * grad_mixed[:, :, None, :]).astype(jnp.bfloat16)
    grad_expert = jax.vmap(place_rows, in_axes=(0, 0, None))(
        grad_picked.reshape(seq_count, seg_len * route_count, model_width), slot_index, slot_total
    )
    grad_expert = grad_expert.reshape(seq_count, EXPERTS, capacity, model_width)
    owner_grads = lax.all_to_all(grad_expert, "seq", split_axis=1, concat_axis=0, tiled=True)
    grad_gate_up, owner_inputs = expert_backward(
        owner_grads, gate_part, up_part, sigmoid_gate, gate_up_weight, down_weight
    )
    grad_down = jnp.einsum(
        "secf,secd->efd", activated, owner_grads, preferred_element_type=jnp.float32
    )
    grad_gu_weight = jnp.einsum(
        "secd,secf->edf", expert_rows, grad_gate_up, preferred_element_type=jnp.float32
    )
    grad_buffers = lax.all_to_all(
        owner_inputs.astype(jnp.bfloat16), "seq", split_axis=0, concat_axis=1, tiled=True
    ).astype(owner_inputs.dtype)
    expert_grads = (
        lax.psum_scatter(
            grad_gu_weight.astype(jnp.bfloat16), "dp", scatter_dimension=1, tiled=True
        ).astype(jnp.float32),
        lax.psum_scatter(
            grad_down.astype(jnp.bfloat16), "dp", scatter_dimension=2, tiled=True
        ).astype(jnp.float32),
    )
    grad_rows = jax.vmap(take_rows)(
        grad_buffers.reshape(seq_count, slot_total, model_width), slot_index
    )
    grad_ffn_rows = jnp.sum(grad_rows.reshape(seq_count, seg_len, route_count, model_width), axis=2)
    router_logit_gradient = jnp.sum(one_hot * grad_chosen[..., None], axis=2).astype(jnp.bfloat16)
    grad_router = jnp.einsum(
        "gyt,gyn->tn",
        feedforward_input_normed,
        router_logit_gradient,
        preferred_element_type=jnp.float32,
    )
    grad_ffn_rows = grad_ffn_rows + jnp.einsum(
        "agc,zc->agz", router_logit_gradient, routing_matrix, preferred_element_type=jnp.float32
    )
    grad_gain_ffn = jnp.sum(grad_ffn_rows * normed_two, axis=(0, 1))
    grad_first = grad_output + norm_back(
        grad_ffn_rows * gain_ffn.astype(jnp.float32), normed_two, scale_two
    )
    branch_gradient = (RESIDUAL_FACTOR * grad_first).astype(jnp.bfloat16)
    grad_out_weight = jnp.einsum(
        "knq,knw->qw", attention_result, branch_gradient, preferred_element_type=jnp.float32
    )
    grad_attended = jnp.einsum(
        "hri,ai->hra", branch_gradient, output_matrix, preferred_element_type=jnp.float32
    )
    grad_attended = grad_attended.reshape(seq_count, seg_len, KV, query_group, HD)
    grad_sum = -jnp.sum(grad_attended * attended_full, axis=-1) / sum_rows
    grad_sum_rows = jnp.transpose(grad_sum, (0, 2, 3, 1))
    grad_unnorm = (grad_attended / sum_rows[..., None]).astype(jnp.bfloat16)
    keys_group, values_group = (
        lax.all_gather(keys_local, "seq", axis=1, tiled=True),
        lax.all_gather(values_local, "seq", axis=1, tiled=True),
    )
    group_len = keys_group.shape[1]
    back_len = 512

    def back_block(grad_queries, block_number):
        offset = block_number * back_len
        key_block = lax.dynamic_slice_in_dim(keys_group, offset, back_len, 1)
        value_block = lax.dynamic_slice_in_dim(values_group, offset, back_len, 1)
        key_pos = offset + jnp.arange(back_len, dtype=jnp.int32)
        scores, keys_four = masked_scores(queries, key_block, query_pos, key_pos, prefix_len)
        exp_weights = jnp.exp(scores - row_max[..., None])
        values_four = value_block.reshape(seq_count, back_len, KV, HD)
        grad_exp = jnp.einsum(
            "sqhgd,skhd->shgqk", grad_unnorm, values_four, preferred_element_type=jnp.float32
        )
        grad_scores = (exp_weights * (grad_exp + grad_sum_rows[..., None])).astype(jnp.bfloat16)
        grad_values = jnp.einsum(
            "shgqk,sqhgd->skhd",
            exp_weights.astype(jnp.bfloat16),
            grad_unnorm,
            preferred_element_type=jnp.float32,
        )
        grad_keys = (
            jnp.einsum(
                "shgqk,sqhgd->skhd", grad_scores, queries, preferred_element_type=jnp.float32
            )
            * SCORE_SCALE
        )
        grad_queries = (
            grad_queries
            + jnp.einsum(
                "shgqk,skhd->sqhgd", grad_scores, keys_four, preferred_element_type=jnp.float32
            )
            * SCORE_SCALE
        )
        return (grad_queries, (grad_keys, grad_values))

    grad_queries, (grad_keys, grad_values) = lax.scan(
        back_block,
        jnp.zeros((seq_count, seg_len, KV, query_group, HD), jnp.float32),
        jnp.arange(group_len // back_len, dtype=jnp.int32),
    )
    grad_keys = jnp.moveaxis(grad_keys, 0, 1).reshape(seq_count, group_len, KV * HD)
    grad_values = jnp.moveaxis(grad_values, 0, 1).reshape(seq_count, group_len, KV * HD)
    keys_owned, values_owned = (
        lax.psum_scatter(
            grad_keys.astype(jnp.bfloat16), "seq", scatter_dimension=1, tiled=True
        ).astype(jnp.float32),
        lax.psum_scatter(
            grad_values.astype(jnp.bfloat16), "seq", scatter_dimension=1, tiled=True
        ).astype(jnp.float32),
    )
    grad_q_rows = rotate(
        grad_queries.reshape(seq_count, seg_len, HEADS, HD), cosine_table, sine_table, -1.0
    )
    grad_k_rows = rotate(
        keys_owned.reshape(seq_count, seg_len, KV, HD), cosine_table, sine_table, -1.0
    )
    projection_gradient = jnp.concatenate(
        [
            grad_q_rows.reshape(seq_count, seg_len, HEADS * HD),
            grad_k_rows.reshape(seq_count, seg_len, KV * HD),
            values_owned,
        ],
        axis=-1,
    ).astype(jnp.bfloat16)
    grad_qkv_weight = jnp.einsum(
        "gyt,gyn->tn",
        attention_input_normed,
        projection_gradient,
        preferred_element_type=jnp.float32,
    )
    grad_normed = jnp.einsum(
        "agc,zc->agz",
        projection_gradient,
        query_key_value_matrix,
        preferred_element_type=jnp.float32,
    )
    grad_gain_attn = jnp.sum(grad_normed * normed_one, axis=(0, 1))
    input_grad = grad_first + norm_back(
        grad_normed * gain_attn.astype(jnp.float32), normed_one, scale_one
    )
    small_grads = (
        lax.psum_scatter(grad_gain_attn, ("dp", "seq"), scatter_dimension=0, tiled=True),
        lax.psum_scatter(grad_qkv_weight, ("dp", "seq"), scatter_dimension=0, tiled=True),
        lax.psum_scatter(grad_out_weight, ("dp", "seq"), scatter_dimension=1, tiled=True),
        lax.psum_scatter(grad_gain_ffn, ("dp", "seq"), scatter_dimension=0, tiled=True),
        lax.psum_scatter(grad_router, ("dp", "seq"), scatter_dimension=0, tiled=True),
    )
    return (
        activations,
        input_grad,
        small_grads[0],
        small_grads[1],
        small_grads[2],
        small_grads[3],
        small_grads[4],
        expert_grads[0],
        expert_grads[1],
    )


def solution(mesh):
    in_specs = (
        P("dp", "seq", None),
        P("dp", "seq", None),
        P("dp"),
        P(("dp", "seq")),
        P(("dp", "seq"), None),
        P(None, ("dp", "seq")),
        P(("dp", "seq")),
        P(("dp", "seq"), None),
        P("seq", "dp", None),
        P("seq", None, "dp"),
        P("dp", "seq", None),
    )
    out_specs = (
        P("dp", "seq", None),
        P("dp", "seq", None),
        P(("dp", "seq")),
        P(("dp", "seq"), None),
        P(None, ("dp", "seq")),
        P(("dp", "seq")),
        P(("dp", "seq"), None),
        P("seq", "dp", None),
        P("seq", None, "dp"),
    )
    return jax.shard_map(body, mesh=mesh, in_specs=in_specs, out_specs=out_specs, check_vma=False)
```

profile of v0, /device:TPU:0, one launch (start us, length us, event | category | flops | bytes accessed | tf_op | source)
XLA Modules:
  0.0 2997.9 jit_solution(10392112490556945349)
XLA Ops:
  10.8 43.4 %all-reduce.5 = (bf16[1536]{0:T(1024)(128)(2,1)S(1)}, bf16[1536]{0:T(1024)(128)(2,1)S(1)}) all-reduce(bf16[1536]{0:T(1024)(128)(2,1)S(1)} %dynamic-update-slice, bf16[1536]{0:T(1024)(128)(2,1)S(1)} %dynamic-update-slice.1), channel_id=1, replica_groups=mesh['dp'=8,'seq'=4] {'dp','seq'}, use_global_device_ids=true, to_apply=%add | all-reduce | flops 3072 | bytes 12288
  56.0 33.5 %all-gather.8.cloned.1.call-done = bf16[1536,2560]{1,0:T(8,128)(2,1)} async-done(((bf16[48,2560]{1,0:T(8,128)(2,1)}), bf16[1536,2560]{1,0:T(8,128)(2,1)}) %all-gather.8.cloned.1.call-update) | async-done | bytes 7864336 | tf_op jit(solution)/shard_map/all_gather | solution.py:77
  127.0 17.3 all-gather.12.cloned.1.call-done
  148.2 43.3 %all-gather.10.cloned.1.call-done = bf16[2,1024,512]{1,2,0:T(8,128)(2,1)} async-done(((bf16[2,256,512]{1,2,0:T(8,128)(2,1)}), bf16[2,1024,512]{1,2,0:T(8,128)(2,1)}) %all-gather.10.cloned.1.call-update) | async-done | bytes 2097168 | tf_op jit(solution)/shard_map/all_gather | solution.py:176
  191.5 77.4 %while.30 = (s32[]{:T(128)}, f32[2,8,3,256]{3,2,1,0:T(4,128)S(1)}, f32[2,8,3,256]{3,2,1,0:T(4,128)S(1)}, f32[2,8,3,256,64]{3,4,2,1,0:T(8,128)}, s32[2]{0:T(128)S...) while((s32[]{:T(128)}, f32[2,8,3,256]{3,2,1,0:T(4,128)S(1)}, ...), condition=%wide.region_4.5_spmd.clone, body=%wide.region_1.4_spmd.clone.sunk | while | flops 1682897152 | bytes 116928800 | solution.py:201
  285.2 28.8 scatter_custom_fusion
  335.3 338.8 %all-to-all-done = bf16[2,16,160,1536]{3,2,0,1:T(8,128)(2,1)} async-done(((bf16[2,16,160,1536]{3,2,0,1:T(8,128)(2,1)}), bf16[2,16,160,1536]{3,2,0,1:T(8,128)(2,1)}, u32[]{:S(2)}, u32[]{:S(2)}) %all-to-all-start) | async-done | bytes 15728672 | tf_op jit(solution)/shard_map/all_to_all | solution.py:226
  674.0 13.4 copy.186
  687.4 20.2 fusion.50
  719.8 15.3 convert_bitcast_fusion.1
  755.4 398.7 %all-gather = bf16[32,48,16]{1,2,0:T(8,128)(2,1)S(1)} all-gather(bf16[1,48,16]{1,2,0:T(8,128)(2,1)S(1)} %convert_bitcast_fusion.4), channel_id=1, replica_groups=mesh['dp'=8,'seq'=4] {'dp','seq'}, dimensions={0}, use_global_device_ids=true | all-gather | bytes 50688 | tf_op jit(solution)/shard_map/all_gather | solution.py:80
  1171.7 91.5 %gather_fusion = bf16[4096,1536]{1,0:T(8,128)(2,1)} fusion(bf16[2,2560,1536]{2,1,0:T(8,128)(2,1)} %bitcast.313, s32[4096]{0:T(1024)S(1)} %bitcast.311), kind=kCustom, calls=%fused_computation | custom fusion | bytes 25198592 | tf_op jit(solution)/shard_map/vmap()/gather | solution.py:63
  1277.6 29.1 scatter_custom_fusion.1
  1314.6 339.0 %all_to_all.60 = bf16[2,16,160,1536]{3,2,0,1:T(8,128)(2,1)S(1)} all-to-all(bf16[2,16,160,1536]{3,2,0,1:T(8,128)(2,1)S(1)} %copy.190), channel_id=1, replica_groups=mesh['dp'=8,'seq'=4] {'seq'}, dimensions={1} | all-to-all | bytes 31457280 | tf_op jit(solution)/shard_map/all_to_all | solution.py:258
  1660.0 21.4 fusion.39
  1681.4 23.2 convert_bitcast_fusion
  1725.1 29.9 fusion.29
  1755.0 307.8 %all-to-all-done.3 = bf16[8,4,160,1536]{3,2,1,0:T(8,128)(2,1)} async-done(((bf16[8,4,160,1536]{3,2,1,0:T(8,128)(2,1)}), bf16[8,4,160,1536]{3,2,1,0:T(8,128)(2,1)}, u32[]{:S(2)}, u32[]{:S(2)}) %all-to-all-start.3) | async-done | bytes 15728672 | tf_op jit(solution)/shard_map/all_to_all | solution.py:268
  2062.8 17.9 copy.194
  2080.6 90.5 %gather_fusion.1 = f32[4096,1536]{1,0:T(8,128)} fusion(f32[2,2560,1536]{2,1,0:T(8,128)} %bitcast.310, s32[4096]{0:T(1024)S(1)} %bitcast.312), kind=kCustom, calls=%fused_computation.1 | custom fusion | bytes 50364416 | tf_op jit(solution)/shard_map/vmap()/gather | solution.py:63
  2192.7 121.7 %while.31 = (s32[]{:T(128)}, f32[2,256,8,3,64]{1,4,3,2,0:T(8,128)}, bf16[2,2,512,8,64]{2,4,3,1,0:T(8,128)(2,1)}, bf16[2,2,512,8,64]{2,4,3,1,0:T(8,128)(2,1)}, s3...) while((s32[]{:T(128)}, f32[2,256,8,3,64]{1,4,3,2,0:T(8,128)}, ...), condition=%wide.region_22.23_spmd.clone, body=%wide.region_21.22_spmd.clone.sunk | while | flops 4092987648 | bytes 144863536 | solution.py:348
  2220.0 15.2 fusion.161
  2280.1 15.2 fusion.161
  2335.0 14.6 bitcast_convert_fusion.1
  2349.7 24.0 bitcast_convert_fusion
  2388.3 23.4 reduce-scatter.12.cloned.1.call-done
  2421.1 91.2 %reduce-scatter.22.cloned.1.call-done = f32[48,16]{1,0:T(8,128)} async-done(((f32[1536,16]{1,0:T(8,128)}), f32[48,16]{1,0:T(8,128)}) %reduce-scatter.22.cloned.1.call-update) | async-done | bytes 3088
  2513.7 62.7 %reduce-scatter.20.cloned.1.call-done = bf16[4,512,192]{1,2,0:T(8,128)(2,1)} async-done(((bf16[4,512,1536]{1,2,0:T(8,128)(2,1)}), bf16[4,512,192]{1,2,0:T(8,128)(2,1)}) %reduce-scatter.20.cloned.1.call-update) | async-done | bytes 786448 | tf_op jit(solution)/shard_map/reduce_scatter | solution.py:275
  2578.9 93.3 %reduce-scatter.18.cloned.1.call-done = bf16[4,192,1024]{2,1,0:T(8,128)(2,1)} async-done(((bf16[4,1536,1024]{2,1,0:T(8,128)(2,1)}), bf16[4,192,1024]{2,1,0:T(8,128)(2,1)}) %reduce-scatter.18.cloned.1.call-update) | async-done | bytes 1572880 | tf_op jit(solution)/shard_map/reduce_scatter | solution.py:272
  2686.3 39.4 %all-reduce.4 = (f32[1536]{0:T(1024)S(1)}, f32[1536]{0:T(1024)S(1)}) all-reduce(f32[1536]{0:T(1024)S(1)} %get-tuple-element.359, f32[1536]{0:T(1024)S(1)} %copy-done.45), channel_id=4, replica_groups=mesh['dp'=8,'seq'=4] {'dp','seq'}, use_global_device_ids=true, to_apply=%region_27.28.clone | all-reduce | flops 3072 | bytes 24576
  2731.7 83.3 %reduce-scatter.16.cloned.1.call-done = f32[1536,48]{0,1:T(8,128)} async-done(((f32[1536,1536]{0,1:T(8,128)}), f32[1536,48]{0,1:T(8,128)}) %reduce-scatter.16.cloned.1.call-update) | async-done | bytes 294928 | tf_op jit(solution)/shard_map/reduce_scatter | solution.py:396
  2815.0 176.2 %reduce-scatter.14.cloned.1.call-done = f32[48,2560]{1,0:T(8,128)} async-done(((f32[1536,2560]{1,0:T(8,128)}), f32[48,2560]{1,0:T(8,128)}) %reduce-scatter.14.cloned.1.call-update) | async-done | bytes 491536 | tf_op jit(solution)/shard_map/reduce_scatter | solution.py:395
  (312 shorter events, 438.1 us)
Async XLA Ops:
  7.2 82.2 %all-gather.8.cloned.1.call-start = ((), (), s32[]{:S(2)}) async-start(), calls=%async_computation.11 | async-start | bytes 8110080 | tf_op jit(solution)/shard_map/all_gather | solution.py:77
  9.0 135.3 %all-gather.12.cloned.1.call-start = ((), (), s32[]{:S(2)}) async-start(), calls=%async_computation.13 | async-start | bytes 2621440 | tf_op jit(solution)/shard_map/all_gather | solution.py:177
  54.1 42.4 %copy-start.43 = (f32[1536]{0:T(1024)}, f32[1536]{0:T(1024)S(1)}, u32[]{:S(2)}) copy-start(f32[1536]{0:T(1024)S(1)} %convert_element_type.177) | copy-start | bytes 18436
  56.0 40.6 %copy-start.46 = (f32[2,256]{1,0:T(2,128)}, f32[2,256]{1,0:T(2,128)S(1)}, u32[]{:S(2)}) copy-start(f32[2,256]{1,0:T(2,128)S(1)} %add_rsqrt_fusion.1) | copy-start | bytes 6148
  99.9 91.6 %all-gather.10.cloned.1.call-start = ((), (), s32[]{:S(2)}) async-start(), calls=%async_computation.12 | async-start | bytes 2621440 | tf_op jit(solution)/shard_map/all_gather | solution.py:176
  100.8 25.6 copy-start.24
  102.4 170.6 %all-gather.14.cloned.1.call-start = ((), (), s32[]{:S(2)}) async-start(), calls=%async_computation.14 | async-start | bytes 4866048 | tf_op jit(solution)/shard_map/all_gather | solution.py:78
  103.2 584.2 %all-gather.16.cloned.1.call-start = ((), (), s32[]{:S(2)}) async-start(), calls=%async_computation.15 | async-start | bytes 14155776 | tf_op jit(solution)/shard_map/all_gather | solution.py:83
  106.6 12.7 copy-start.50
  106.6 12.8 copy-start.49
  126.8 64.7 %copy-start.34 = (s32[2]{0:T(128)S(1)}, s32[2]{0:T(128)}, u32[]{:S(2)}) copy-start(s32[2]{0:T(128)} %param.17) | copy-start | bytes 28
  327.2 346.8 %all-to-all-start = ((bf16[2,16,160,1536]{3,2,0,1:T(8,128)(2,1)}), bf16[2,16,160,1536]{3,2,0,1:T(8,128)(2,1)}, u32[]{:S(2)}, u32[]{:S(2)}) async-start(bf16[2,16,160,1536]{3,2,0,1:T(8,128)(2,1)} %copy.184), calls=%async_computation | async-start | bytes 31457280 | tf_op jit(solution)/shard_map/all_to_all | solution.py:226
  334.2 385.6 %all-gather.18.cloned.1.call-start = ((), (), s32[]{:S(2)}) async-start(), calls=%async_computation.16 | async-start | bytes 7077888 | tf_op jit(solution)/shard_map/all_gather | solution.py:84
  748.3 406.0 %copy-start.40 = (s32[1,16,2,128]{3,2,1,0:T(2,128)S(1)}, s32[1,16,2,128]{3,2,1,0:T(2,128)}, u32[]{:S(2)}) copy-start(s32[1,16,2,128]{3,2,1,0:T(2,128)} %get-tuple-element.415) | copy-start | bytes 49156
  748.3 410.2 %all-to-all-start.1 = ((bf16[8,4,160,1536]{3,2,1,0:T(8,128)(2,1)}), bf16[8,4,160,1536]{3,2,1,0:T(8,128)(2,1)}, u32[]{:S(2)}, u32[]{:S(2)}) async-start(bf16[8,4,160,1536]{3,2,1,0:T(8,128)(2,1)} %copy.187), calls=%async_computation.1 | async-start | bytes 31457280 | tf_op jit(solution)/shard_map/all_to_all | solution.py:230
  1717.8 345.0 %all-to-all-start.3 = ((bf16[8,4,160,1536]{3,2,1,0:T(8,128)(2,1)}), bf16[8,4,160,1536]{3,2,1,0:T(8,128)(2,1)}, u32[]{:S(2)}, u32[]{:S(2)}) async-start(bf16[8,4,160,1536]{3,2,1,0:T(8,128)(2,1)} %copy.193), calls=%async_computation.3 | async-start | bytes 31457280 | tf_op jit(solution)/shard_map/all_to_all | solution.py:268
  1724.8 661.8 %reduce-scatter.10.cloned.1.call-start = ((), (), s32[]{:S(2)}) async-start(), calls=%async_computation.17 | async-start | bytes 2621440 | tf_op jit(solution)/shard_map/reduce_scatter | solution.py:356
  1725.1 458.1 %copy-start.36 = (bf16[2,256,16]{1,2,0:T(8,128)(2,1)}, bf16[2,256,16]{1,2,0:T(8,128)(2,1)S(1)}, u32[]{:S(2)}) copy-start(bf16[2,256,16]{1,2,0:T(8,128)(2,1)S(1)} %select_reduce_fusion) | copy-start | bytes 49156
  2171.2 12.0 copy-start.28
  2171.2 12.0 copy-start.39
  2171.2 12.0 copy-start.42
  2320.9 90.8 %reduce-scatter.12.cloned.1.call-start = ((), (), s32[]{:S(2)}) async-start(), calls=%async_computation.18 | async-start | bytes 2621440 | tf_op jit(solution)/shard_map/reduce_scatter | solution.py:359
  2333.2 179.1 %reduce-scatter.22.cloned.1.call-start = ((), (), s32[]{:S(2)}) async-start(), calls=%async_computation.23 | async-start | bytes 811008
  2334.9 241.4 %reduce-scatter.20.cloned.1.call-start = ((), (), s32[]{:S(2)}) async-start(), calls=%async_computation.22 | async-start | bytes 7077888 | tf_op jit(solution)/shard_map/reduce_scatter | solution.py:275
  2349.6 322.6 %reduce-scatter.18.cloned.1.call-start = ((), (), s32[]{:S(2)}) async-start(), calls=%async_computation.21 | async-start | bytes 14155776 | tf_op jit(solution)/shard_map/reduce_scatter | solution.py:272
  2373.7 441.2 %reduce-scatter.16.cloned.1.call-start = ((), (), s32[]{:S(2)}) async-start(), calls=%async_computation.20 | async-start | bytes 9732096 | tf_op jit(solution)/shard_map/reduce_scatter | solution.py:396
  2382.5 608.7 %reduce-scatter.14.cloned.1.call-start = ((), (), s32[]{:S(2)}) async-start(), calls=%async_computation.19 | async-start | bytes 16220160 | tf_op jit(solution)/shard_map/reduce_scatter | solution.py:395
  2386.6 25.1 copy-start.17
  2386.6 25.1 copy-start.44
  2386.6 25.1 copy-start.47
  2388.3 32.8 %copy-start.26 = (bf16[2,256,512]{2,1,0:T(8,128)(2,1)}, bf16[2,256,512]{2,1,0:T(8,128)(2,1)S(1)}, u32[]{:S(2)}) copy-start(bf16[2,256,512]{2,1,0:T(8,128)(2,1)S(1)} %copy.203) | copy-start | bytes 1572868
  2675.7 51.2 %copy-start.13 = (f32[2,256,1536]{2,1,0:T(8,128)S(1)}, f32[2,256,1536]{2,1,0:T(8,128)}, u32[]{:S(2)}) copy-start(f32[2,256,1536]{2,1,0:T(8,128)} %copy-done.11) | copy-start | bytes 9437188
  (41 other events, 216.2 us)
Sparse Core Ops, SparseCore 0:
  11.4 78.0 all-gather.7
  100.0 44.2 all-gather.11
  146.4 45.0 all-gather.9
  194.7 61.7 all-gather.13
  258.9 70.2 all-gather.15
  336.6 46.7 all-gather.17
  2321.0 44.8 reduce-scatter.9
  2368.8 42.8 reduce-scatter.11
  2416.8 95.4 reduce-scatter.21
  2515.5 60.7 reduce-scatter.19
  2579.9 92.2 reduce-scatter.17
  2678.5 136.4 reduce-scatter.15
  2821.6 169.5 reduce-scatter.13
where the time goes:
time: 3010 us; the launch traced here: 3000 us
  waiting for transfers between devices  1270 us (42%)
  blocking collectives  820 us (27%)
  local copies, waits for them, and re-layouts  411 us (14%)
  matrix products  322 us (11%)
  other arithmetic  134 us (4%)
    all_gather x1, blocking collectives, fetch_weights(): lax.all_gather(w_router.astype(jnp.bfloat16), ('dp', 'seq'), axis=0, tile...  399 us
    all_to_all x1, blocking collectives, body(): lax.all_to_all(grad_expert, 'seq', split_axis=1, concat_axis=0, tiled=True)  339 us
    all_to_all x1, waiting for transfers between devices, body(): lax.all_to_all(buffers, 'seq', split_axis=1, concat_axis=0, tiled=True)  339 us
    all_to_all x1, waiting for transfers between devices, body(): lax.all_to_all(owner_inputs.astype(jnp.bfloat16), 'seq', split_axis=0, co...  308 us
    gather x2, local copies, waits for them, and re-layouts, take_rows(): return source[slot_row]  182 us
    reduce_scatter x1, waiting for transfers between devices, body(): lax.psum_scatter(grad_qkv_weight, ('dp', 'seq'), scatter_dimension=0, til...  176 us
    reduce_scatter x1, waiting for transfers between devices, body(): lax.psum_scatter(grad_gu_weight.astype(jnp.bfloat16), 'dp', scatter_dimen...  93.3 us
    unnamed x14, waiting for transfers between devices  91.4 us
  transfers between devices with their start and end apart: 16, of which 11 were waited for; matrix products, arithmetic and copies ran while one was open for 11% of the time, Pallas kernels for 0%

commit v1 on v0

v1 whole, which is shorter than its diff:
```python
import functools

import jax
import jax.numpy as jnp
from jax import lax
from jax.experimental import pallas as pl
from jax.experimental.pallas import tpu as pltpu
from jax.sharding import PartitionSpec as P

HEADS = 24
KV = 8
HD = 64
EXPERTS = 16
EPSILON = 1e-06
SCORE_SCALE = 0.015625
RESIDUAL_FACTOR = 0.22
ROTARY_BASE = 10000.0
NEGATIVE_FILL = -1e30
BF = jnp.bfloat16
F32 = jnp.float32
LANES = 128
GROUP = HEADS // KV
PAIR_Q = 2 * GROUP * HD
VMEM_LIMIT = 62 * 1024 * 1024


def nt(a, b):
    return lax.dot_general(a, b, (((1,), (1,)), ((), ())), preferred_element_type=F32)


def nn(a, b):
    return lax.dot_general(a, b, (((1,), (0,)), ((), ())), preferred_element_type=F32)


def tn(a, b):
    return lax.dot_general(a, b, (((0,), (0,)), ((), ())), preferred_element_type=F32)


def rotary_tables(seg_len):
    half = HD // 2
    positions = lax.axis_index("seq") * seg_len + jnp.arange(seg_len, dtype=jnp.int32)
    inverse = ROTARY_BASE ** (-(jnp.arange(half, dtype=F32) * 2.0 / HD))
    angles = positions.astype(F32)[:, None] * inverse[None, :]
    cosine = jnp.tile(jnp.cos(angles), (1, LANES // half))
    sine = jnp.sin(angles)
    sine = jnp.concatenate([-sine, sine] * (LANES // HD), axis=1)
    return cosine, sine


def rotate_lanes(values, cosine, sine):
    lane = lax.broadcasted_iota(jnp.int32, values.shape, 1)
    half = HD // 2
    swapped = jnp.where(
        lane % HD < half, pltpu.roll(values, LANES - half, 1), pltpu.roll(values, half, 1)
    )
    return values * cosine + swapped * sine


def rope_kernel(x_ref, cos_ref, sin_ref, q_ref, kv_ref):
    cosine, sine = cos_ref[...], sin_ref[...]
    q_cols, kv_cols = HEADS * HD, KV * HD
    for c in range(q_cols // LANES):
        cols = pl.ds(c * LANES, LANES)
        q_ref[0, :, cols] = rotate_lanes(x_ref[0, :, cols], cosine, sine).astype(BF)
    for c in range(kv_cols // LANES):
        cols = pl.ds(c * LANES, LANES)
        source = x_ref[0, :, pl.ds(q_cols + c * LANES, LANES)]
        kv_ref[0, 0, :, cols] = rotate_lanes(source, cosine, sine).astype(BF)
        kv_ref[1, 0, :, cols] = x_ref[0, :, pl.ds(q_cols + kv_cols + c * LANES, LANES)].astype(BF)


def rope(qkv, cosine, sine):
    seqs, seg_len, width = qkv.shape
    return pl.pallas_call(
        rope_kernel,
        grid=(seqs,),
        in_specs=[
            pl.BlockSpec((1, seg_len, width), lambda s: (s, 0, 0)),
            pl.BlockSpec((seg_len, LANES), lambda s: (0, 0)),
            pl.BlockSpec((seg_len, LANES), lambda s: (0, 0)),
        ],
        out_specs=[
            pl.BlockSpec((1, seg_len, HEADS * HD), lambda s: (s, 0, 0)),
            pl.BlockSpec((2, 1, seg_len, KV * HD), lambda s: (0, s, 0, 0)),
        ],
        out_shape=[
            jax.ShapeDtypeStruct((seqs, seg_len, HEADS * HD), BF),
            jax.ShapeDtypeStruct((2, seqs, seg_len, KV * HD), BF),
        ],
        name="rope",
    )(qkv, cosine, sine)


def unrope_kernel(dq_ref, dkv_ref, cos_ref, sin_ref, out_ref):
    cosine, sine = cos_ref[...], -sin_ref[...]
    q_cols, kv_cols = HEADS * HD, KV * HD
    for c in range(q_cols // LANES):
        cols = pl.ds(c * LANES, LANES)
        out_ref[0, :, cols] = rotate_lanes(dq_ref[0, :, cols], cosine, sine).astype(BF)
    for c in range(kv_cols // LANES):
        cols = pl.ds(c * LANES, LANES)
        keys = dkv_ref[0, 0, :, cols].astype(F32)
        out_ref[0, :, pl.ds(q_cols + c * LANES, LANES)] = rotate_lanes(keys, cosine, sine).astype(BF)
        out_ref[0, :, pl.ds(q_cols + kv_cols + c * LANES, LANES)] = dkv_ref[1, 0, :, cols].astype(BF)


def unrope(dq, dkv, cosine, sine):
    seqs, seg_len, q_cols = dq.shape
    kv_cols = KV * HD
    width = q_cols + 2 * kv_cols
    return pl.pallas_call(
        unrope_kernel,
        grid=(seqs,),
        in_specs=[
            pl.BlockSpec((1, seg_len, q_cols), lambda s: (s, 0, 0)),
            pl.BlockSpec((2, 1, seg_len, kv_cols), lambda s: (0, s, 0, 0)),
            pl.BlockSpec((seg_len, LANES), lambda s: (0, 0)),
            pl.BlockSpec((seg_len, LANES), lambda s: (0, 0)),
        ],
        out_specs=pl.BlockSpec((1, seg_len, width), lambda s: (s, 0, 0)),
        out_shape=jax.ShapeDtypeStruct((seqs, seg_len, width), BF),
        name="unrope",
    )(dq, dkv, cosine, sine)


def spread_heads(source, scratch, rows, scale=None):
    lane = lax.broadcasted_iota(jnp.int32, (rows, LANES), 1)
    for head in range(2 * GROUP):
        odd = head >= GROUP
        group, high = divmod(head, 2)
        values = source(group)
        if bool(high) != odd:
            values = pltpu.roll(values, HD, 1)
        keep = lane >= HD if odd else lane < HD
        values = jnp.where(keep, values, jnp.zeros_like(values))
        if scale is not None:
            values = values * scale
        scratch[pl.ds(head * rows, rows), :] = values.astype(scratch.dtype)


def gather_heads(scratch, rows, sink):
    lane = lax.broadcasted_iota(jnp.int32, (rows, LANES), 1)
    for group in range(GROUP):
        parts = []
        for high in range(2):
            head = 2 * group + high
            odd = head >= GROUP
            values = scratch[pl.ds(head * rows, rows), :]
            if bool(high) != odd:
                values = pltpu.roll(values, HD, 1)
            parts.append(values)
        sink(group, jnp.where(lane < HD, parts[0], parts[1]))


def query_limits(info_ref, rows, seqs):
    prefix = info_ref[pl.program_id(0)]
    start = info_ref[seqs] * rows
    position = start + lax.broadcasted_iota(jnp.int32, (rows, 1), 0)
    return jnp.where(position < prefix, prefix, position + 1)


def attention_kernel(seqs, info_ref, q_ref, k_ref, v_ref, o_ref, ml_ref, q_all, o_all):
    rows = q_ref.shape[1]
    keys = k_ref.shape[0] * k_ref.shape[3]
    limit = query_limits(info_ref, rows, seqs)
    spread_heads(lambda g: q_ref[0, :, pl.ds(g * LANES, LANES)].astype(F32), q_all, rows, SCORE_SCALE)
    lane = lax.broadcasted_iota(jnp.int32, (rows, LANES), 1)

    def one_head(head, ml):
        q = q_all[pl.ds(pl.multiple_of(head * rows, rows), rows), :]
        k = k_ref[:, 0, 0].reshape(keys, LANES)
        v = v_ref[:, 0, 0].reshape(keys, LANES)
        scores = nt(q, k)
        position = lax.broadcasted_iota(jnp.int32, (rows, keys), 1)
        scores = jnp.where(position < limit, scores, NEGATIVE_FILL)
        top = jnp.max(scores, axis=1, keepdims=True)
        weights = jnp.exp(scores - top)
        total = jnp.sum(weights, axis=1, keepdims=True)
        mixed = nn(weights.astype(BF), v)
        o_all[pl.ds(pl.multiple_of(head * rows, rows), rows), :] = mixed / total
        ml = jnp.where(lane == head, top, ml)
        return jnp.where(lane == head + HD, total, ml)

    ml_ref[0, 0] = lax.fori_loop(0, 2 * GROUP, one_head, jnp.zeros((rows, LANES), F32))

    def sink(group, values):
        o_ref[0, :, pl.ds(group * LANES, LANES)] = values.astype(BF)

    gather_heads(o_all, rows, sink)


def kv_specs(pieces, seg_len):
    return [
        pl.BlockSpec((pieces, 1, 1, seg_len, LANES), lambda s, p, info: (0, 0, s, 0, p)),
        pl.BlockSpec((pieces, 1, 1, seg_len, LANES), lambda s, p, info: (0, 1, s, 0, p)),
    ]


def attention(info, queries, kv_all):
    seqs, seg_len, width = queries.shape
    pieces = kv_all.shape[0]
    head_rows = 2 * GROUP * seg_len
    pairs = KV // 2
    return pl.pallas_call(
        functools.partial(attention_kernel, seqs),
        grid_spec=pltpu.PrefetchScalarGridSpec(
            num_scalar_prefetch=1,
            grid=(seqs, pairs),
            in_specs=[pl.BlockSpec((1, seg_len, PAIR_Q), lambda s, p, info: (s, 0, p))]
            + kv_specs(pieces, seg_len),
            out_specs=[
                pl.BlockSpec((1, seg_len, PAIR_Q), lambda s, p, info: (s, 0, p)),
                pl.BlockSpec((1, 1, seg_len, LANES), lambda s, p, info: (s, p, 0, 0)),
            ],
            scratch_shapes=[
                pltpu.VMEM((head_rows, LANES), BF),
                pltpu.VMEM((head_rows, LANES), F32),
            ],
        ),
        out_shape=[
            jax.ShapeDtypeStruct((seqs, seg_len, width), BF),
            jax.ShapeDtypeStruct((seqs, pairs, seg_len, LANES), F32),
        ],
        compiler_params=pltpu.CompilerParams(vmem_limit_bytes=VMEM_LIMIT),
        name="attention",
    )(info, queries, kv_all, kv_all)


def attention_back_kernel(
    seqs, info_ref, q_ref, k_ref, v_ref, o_ref, g_ref, ml_ref, dq_ref, dkv_ref,
    q_all, o_all, g_all, dq_all, dk_all, dv_all,
):
    rows = q_ref.shape[1]
    pieces, seg_len = k_ref.shape[0], k_ref.shape[3]
    keys = pieces * seg_len
    limit = query_limits(info_ref, rows, seqs)

    def columns(ref):
        return lambda g: ref[0, :, pl.ds(g * LANES, LANES)].astype(F32)

    spread_heads(columns(q_ref), q_all, rows, SCORE_SCALE)
    spread_heads(columns(o_ref), o_all, rows)
    spread_heads(columns(g_ref), g_all, rows)
    lane = lax.broadcasted_iota(jnp.int32, (rows, LANES), 1)
    dk_all[...] = jnp.zeros_like(dk_all)
    dv_all[...] = jnp.zeros_like(dv_all)
    ml = ml_ref[0, 0]

    def one_head(head, carry):
        part = pl.ds(pl.multiple_of(head * rows, rows), rows)
        q = q_all[part, :]
        k = k_ref[:, 0, 0].reshape(keys, LANES)
        v = v_ref[:, 0, 0].reshape(keys, LANES)
        top = jnp.sum(jnp.where(lane == head, ml, 0.0), axis=1, keepdims=True)
        total = jnp.sum(jnp.where(lane == head + HD, ml, 0.0), axis=1, keepdims=True)
        grad = g_all[part, :]
        grad_total = -jnp.sum(grad * o_all[part, :], axis=1, keepdims=True) / total
        grad_mix = (grad / total).astype(BF)
        scores = nt(q, k)
        position = lax.broadcasted_iota(jnp.int32, (rows, keys), 1)
        scores = jnp.where(position < limit, scores, NEGATIVE_FILL)
        weights = jnp.exp(scores - top)
        grad_weights = nt(grad_mix, v) + grad_total
        grad_scores = (weights * grad_weights).astype(BF)
        dq_all[part, :] = nn(grad_scores, k) * SCORE_SCALE
        dk_all[...] += tn(grad_scores, q)
        dv_all[...] += tn(weights.astype(BF), grad_mix)
        return carry

    lax.fori_loop(0, 2 * GROUP, one_head, 0)

    def sink(group, values):
        dq_ref[0, :, pl.ds(group * LANES, LANES)] = values

    gather_heads(dq_all, rows, sink)
    dkv_ref[:, 0, 0] = dk_all[...].astype(BF).reshape(pieces, seg_len, LANES)
    dkv_ref[:, 1, 0] = dv_all[...].astype(BF).reshape(pieces, seg_len, LANES)


def attention_back(info, queries, kv_all, attended, grads, ml):
    seqs, seg_len, width = queries.shape
    pieces = kv_all.shape[0]
    head_rows = 2 * GROUP * seg_len
    pairs = KV // 2
    rows_spec = pl.BlockSpec((1, seg_len, PAIR_Q), lambda s, p, info: (s, 0, p))
    return pl.pallas_call(
        functools.partial(attention_back_kernel, seqs),
        grid_spec=pltpu.PrefetchScalarGridSpec(
            num_scalar_prefetch=1,
            grid=(seqs, pairs),
            in_specs=[rows_spec]
            + kv_specs(pieces, seg_len)
            + [
                rows_spec,
                rows_spec,
                pl.BlockSpec((1, 1, seg_len, LANES), lambda s, p, info: (s, p, 0, 0)),
            ],
            out_specs=[
                rows_spec,
                pl.BlockSpec((pieces, 2, 1, seg_len, LANES), lambda s, p, info: (0, 0, s, 0, p)),
            ],
            scratch_shapes=[
                pltpu.VMEM((head_rows, LANES), BF),
                pltpu.VMEM((head_rows, LANES), F32),
                pltpu.VMEM((head_rows, LANES), F32),
                pltpu.VMEM((head_rows, LANES), F32),
                pltpu.VMEM((pieces * seg_len, LANES), F32),
                pltpu.VMEM((pieces * seg_len, LANES), F32),
            ],
        ),
        out_shape=[
            jax.ShapeDtypeStruct((seqs, seg_len, width), F32),
            jax.ShapeDtypeStruct((pieces, 2, seqs, seg_len, KV * HD), BF),
        ],
        compiler_params=pltpu.CompilerParams(vmem_limit_bytes=VMEM_LIMIT),
        name="attention_back",
    )(info, queries, kv_all, kv_all, attended, grads, ml)


def experts_kernel(
    h_ref, ht_ref, go_ref, got_ref, gate_ref, w_ref,
    out_ref, dh_ref, dgate_ref, gw_ref,
    out_acc, dh_acc, act_all, dgu_all,
):
    expert = pl.program_id(0)
    tokens, width = h_ref.shape
    slots, slice_len = w_ref.shape[0], w_ref.shape[2]
    hidden = act_all.shape[1]
    rows = min(512, tokens)
    wide = 768
    wide_slots = wide // slice_len

    @pl.when(expert == 0)
    def _():
        out_acc[...] = jnp.zeros_like(out_acc)
        dh_acc[...] = jnp.zeros_like(dh_acc)
        dgate_ref[...] = jnp.zeros_like(dgate_ref)

    def weight(cols):
        return w_ref[:, 0, :, cols].reshape(width, cols.size)

    def token_block(block, carry):
        part = pl.ds(pl.multiple_of(block * rows, rows), rows)
        lane = lax.broadcasted_iota(jnp.int32, (rows, LANES), 1)
        gate = jnp.sum(jnp.where(lane == expert, gate_ref[part, :], 0.0), axis=1, keepdims=True)
        h = h_ref[part, :]
        g = nn(h, weight(pl.ds(0, hidden)))
        up = nn(h, weight(pl.ds(hidden, hidden)))
        da = nn(go_ref[part, :], weight(pl.ds(2 * hidden, hidden))) * RESIDUAL_FACTOR
        sig = 1.0 / (1.0 + jnp.exp(-g))
        silu = g * sig
        act = silu * up
        act_all[part, :] = (gate * act).astype(BF)
        dgate = jnp.sum(act * da, axis=1, keepdims=True)
        dgate_ref[part, :] = jnp.where(lane == expert, dgate, dgate_ref[part, :])
        dact = gate * da
        dgu_all[part, pl.ds(0, hidden)] = (dact * up * (sig * (1.0 + g * (1.0 - sig)))).astype(BF)
        dgu_all[part, pl.ds(hidden, hidden)] = (dact * silu).astype(BF)
        for n in range(width // wide):
            some = pl.ds(n * wide_slots, wide_slots)
            cols = pl.ds(n * wide, wide)
            down = w_ref[some, 0, :, pl.ds(2 * hidden, hidden)].reshape(wide, hidden)
            out_acc[part, cols] += nt(act_all[part, :], down)
            gate_up = w_ref[some, 0, :, pl.ds(0, 2 * hidden)].reshape(wide, 2 * hidden)
            dh_acc[part, cols] += nt(dgu_all[part, :], gate_up)
        return carry

    lax.fori_loop(0, tokens // rows, token_block, 0)

    tall = 384
    tall_slots = tall // slice_len

    def weight_block(block, carry):
        part = pl.ds(pl.multiple_of(block * tall, tall), tall)
        some = pl.ds(block * tall_slots, tall_slots)
        gw_gate_up = nn(ht_ref[part, :], dgu_all[...]).astype(BF)
        gw_ref[some, 0, :, pl.ds(0, 2 * hidden)] = gw_gate_up.reshape(
            tall_slots, slice_len, 2 * hidden
        )
        gw_down = (nn(got_ref[part, :], act_all[...]) * RESIDUAL_FACTOR).astype(BF)
        gw_ref[some, 0, :, pl.ds(2 * hidden, hidden)] = gw_down.reshape(
            tall_slots, slice_len, hidden
        )
        return carry

    lax.fori_loop(0, width // tall, weight_block, 0)

    @pl.when(expert == pl.num_programs(0) - 1)
    def _():
        out_ref[...] = out_acc[...].astype(BF)
        dh_ref[...] = dh_acc[...].astype(BF)


def experts_pass(h, ht, go, got, gates, weights):
    tokens, width = h.shape
    slots, experts, slice_len, packed = weights.shape
    hidden = packed // 3
    one = pl.Buffered(1)
    fixed = lambda shape: pl.BlockSpec(shape, lambda e: (0, 0), pipeline_mode=one)
    moving = pl.BlockSpec((slots, 1, slice_len, packed), lambda e: (0, e, 0, 0))
    flops = 2 * 9 * tokens * width * hidden * experts
    return pl.pallas_call(
        experts_kernel,
        grid=(experts,),
        in_specs=[
            fixed((tokens, width)),
            fixed((width, tokens)),
            fixed((tokens, width)),
            fixed((width, tokens)),
            fixed((tokens, LANES)),
            moving,
        ],
        out_specs=[
            fixed((tokens, width)),
            fixed((tokens, width)),
            fixed((tokens, LANES)),
            moving,
        ],
        out_shape=[
            jax.ShapeDtypeStruct((tokens, width), BF),
            jax.ShapeDtypeStruct((tokens, width), BF),
            jax.ShapeDtypeStruct((tokens, LANES), F32),
            jax.ShapeDtypeStruct(weights.shape, BF),
        ],
        scratch_shapes=[
            pltpu.VMEM((tokens, width), F32),
            pltpu.VMEM((tokens, width), F32),
            pltpu.VMEM((tokens, hidden), BF),
            pltpu.VMEM((tokens, 2 * hidden), BF),
        ],
        compiler_params=pltpu.CompilerParams(vmem_limit_bytes=VMEM_LIMIT),
        cost_estimate=pl.CostEstimate(
            flops=flops, transcendentals=tokens * hidden * experts, bytes_accessed=4 * weights.size
        ),
        name="experts",
    )(h, ht, go, got, gates, weights)


def norm_back(grad_norm, normed, scale_row):
    return scale_row * (grad_norm - normed * jnp.mean(grad_norm * normed, axis=-1, keepdims=True))


def body(
    tokens_in, expert_ids, prefix_len, attn_gain, w_qkv, w_out, ffn_gain, w_router,
    w_gate_up, w_down, out_grad,
):
    seqs, seg_len, width = tokens_in.shape
    tokens = seqs * seg_len
    n_dp, n_seq = lax.axis_size("dp"), lax.axis_size("seq")
    everyone = ("dp", "seq")
    rounds = n_seq // 2
    held = w_gate_up.shape[0]
    me = lax.axis_index("seq")

    def swap(values, bit):
        return lax.ppermute(values, "seq", [(i, i ^ bit) for i in range(n_seq)])

    gains = lax.all_gather(jnp.stack([attn_gain, ffn_gain]).astype(BF), everyone, axis=1, tiled=True)
    gain_attn, gain_ffn = gains[0].astype(F32), gains[1].astype(F32)
    qkv_matrix = lax.all_gather(w_qkv.astype(BF), everyone, axis=0, tiled=True)
    packed = jnp.concatenate([w_gate_up.astype(BF), jnp.swapaxes(w_down, 1, 2).astype(BF)], axis=2)
    packed_rounds = [packed] + [swap(packed, 2 * r) for r in range(1, rounds)]
    out_matrix = lax.all_gather(w_out.T.astype(BF), everyone, axis=0, tiled=True)
    router_matrix = lax.all_gather(w_router.astype(BF), everyone, axis=0, tiled=True)
    expert_rounds = [lax.all_gather(p, "dp", axis=0) for p in packed_rounds]

    go_mine = out_grad.reshape(tokens, width)
    go = jnp.concatenate([go_mine, swap(go_mine, 1)], axis=0)
    ids_mine = expert_ids.reshape(tokens, -1)
    ids = jnp.concatenate([ids_mine, swap(ids_mine, 1)], axis=0)
    got = go.T

    x = tokens_in.reshape(tokens, width).astype(F32)
    scale_one = lax.rsqrt(jnp.mean(x * x, axis=-1, keepdims=True) + EPSILON)
    normed_one = x * scale_one
    h1 = (normed_one * gain_attn).astype(BF)
    qkv = nn(h1, qkv_matrix)
    cosine, sine = rotary_tables(seg_len)
    queries, kv_mine = rope(qkv.reshape(seqs, seg_len, -1), cosine, sine)
    kv_all = lax.all_gather(kv_mine, "seq", axis=0)
    info = jnp.concatenate([prefix_len, me[None].astype(jnp.int32)])
    attended, ml = attention(info, queries, kv_all)
    att = attended.reshape(tokens, width)
    r1 = x + RESIDUAL_FACTOR * nt(att, out_matrix)
    scale_two = lax.rsqrt(jnp.mean(r1 * r1, axis=-1, keepdims=True) + EPSILON)
    normed_two = r1 * scale_two
    h2_mine = (normed_two * gain_ffn).astype(BF)

    h2 = jnp.concatenate([h2_mine, swap(h2_mine, 1)], axis=0)
    h2t = h2.T
    logits = nn(h2, router_matrix)
    routed = jnp.any(ids[:, :, None] == jnp.arange(EXPERTS, dtype=jnp.int32), axis=1)
    chosen = jnp.where(routed, logits, NEGATIVE_FILL)
    chosen = jnp.exp(chosen - jnp.max(chosen, axis=-1, keepdims=True))
    chosen = jnp.where(routed, chosen, 0.0)
    gates = chosen / jnp.sum(chosen, axis=-1, keepdims=True)

    out_part = 0.0
    dh_part = 0.0
    dgates = jnp.zeros((tokens, EXPERTS), F32)
    dgates_away = []
    weight_grads = []
    for r in range(rounds):
        local = lax.dynamic_slice_in_dim(gates, (me ^ (2 * r)) * held, held, 1)
        local = jnp.pad(local, ((0, 0), (0, LANES - held)))
        out_r, dh_r, dgate_r, gw_r = experts_pass(h2, h2t, go, got, local, expert_rounds[r])
        out_part = out_part + out_r.astype(F32)
        dh_part = dh_part + dh_r.astype(F32)
        dgates = lax.dynamic_update_slice_in_dim(
            dgates, dgate_r[:tokens, :held], (me ^ (2 * r)) * held, 1
        )
        dgates_away.append(dgate_r[tokens:, :held])
        weight_grads.append(gw_r)
    dh_from = swap(dh_part[tokens:].astype(BF), 1).astype(F32)
    dgates_from = swap(jnp.concatenate(dgates_away, axis=1), 1)
    out_from = swap(out_part[tokens:].astype(BF), 1).astype(F32)
    for r in range(rounds):
        dgates = lax.dynamic_update_slice_in_dim(
            dgates, dgates_from[:, r * held : (r + 1) * held], (me ^ 1 ^ (2 * r)) * held, 1
        )
    activations = (r1 + RESIDUAL_FACTOR * (out_part[:tokens] + out_from)).astype(BF)

    own_gates = gates[:tokens]
    dlogits = own_gates * (dgates - jnp.sum(own_gates * dgates, axis=-1, keepdims=True))
    dlogits = dlogits.astype(BF)
    grad_router = tn(h2_mine, dlogits)
    dh2 = dh_part[:tokens] + dh_from + nt(dlogits, router_matrix)
    grad_gain_ffn = jnp.sum(dh2 * normed_two, axis=0)
    dr1 = go_mine.astype(F32) + norm_back(dh2 * gain_ffn, normed_two, scale_two)
    dbr = (RESIDUAL_FACTOR * dr1).astype(BF)
    grad_out = tn(dbr, att).astype(BF)
    datt = nn(dbr, out_matrix)

    dq, dkv = attention_back(
        info, queries, kv_all, attended, datt.reshape(seqs, seg_len, width), ml
    )
    dkv = lax.psum_scatter(dkv, "seq", scatter_dimension=0)
    dqkv = unrope(dq, dkv, cosine, sine).reshape(tokens, -1)
    grad_qkv = tn(h1, dqkv).astype(BF)
    dh1 = nt(dqkv, qkv_matrix)
    grad_gain_attn = jnp.sum(dh1 * normed_one, axis=0)
    input_grad = dr1 + norm_back(dh1 * gain_attn, normed_one, scale_one)

    scattered = [lax.psum_scatter(g, "dp", scatter_dimension=0).astype(F32) for g in weight_grads]
    mine = scattered[0]
    for r in range(1, rounds):
        mine = mine + swap(scattered[r].astype(BF), 2 * r).astype(F32)
    hidden = w_down.shape[1]
    grad_gate_up = mine[:, :, : 2 * hidden]
    grad_down = jnp.swapaxes(mine[:, :, 2 * hidden :], 1, 2)
    grad_out = lax.psum_scatter(grad_out, everyone, scatter_dimension=0, tiled=True).astype(F32).T
    grad_qkv = lax.psum_scatter(grad_qkv, everyone, scatter_dimension=0, tiled=True).astype(F32)
    small = jnp.concatenate([grad_gain_attn[:, None], grad_gain_ffn[:, None], grad_router], axis=1)
    small = lax.psum_scatter(small, everyone, scatter_dimension=0, tiled=True)
    return (
        activations.reshape(tokens_in.shape),
        input_grad.reshape(tokens_in.shape),
        small[:, 0],
        grad_qkv,
        grad_out,
        small[:, 1],
        small[:, 2:],
        grad_gate_up,
        grad_down,
    )


def solution(mesh):
    in_specs = (
        P("dp", "seq", None),
        P("dp", "seq", None),
        P("dp"),
        P(("dp", "seq")),
        P(("dp", "seq"), None),
        P(None, ("dp", "seq")),
        P(("dp", "seq")),
        P(("dp", "seq"), None),
        P("seq", "dp", None),
        P("seq", None, "dp"),
        P("dp", "seq", None),
    )
    out_specs = (
        P("dp", "seq", None),
        P("dp", "seq", None),
        P(("dp", "seq")),
        P(("dp", "seq"), None),
        P(None, ("dp", "seq")),
        P(("dp", "seq")),
        P(("dp", "seq"), None),
        P("seq", "dp", None),
        P("seq", None, "dp"),
    )
    return jax.shard_map(body, mesh=mesh, in_specs=in_specs, out_specs=out_specs, check_vma=False)
```

time: 3010 us -> 1540 us (0.51)
  blocking collectives: 820 us -> 169 us
  waiting for transfers between devices: 1270 us -> 905 us
  local copies, waits for them, and re-layouts: 411 us -> 75.2 us
  matrix products: 322 us -> 58.4 us
  Pallas kernels: 0 us -> 257 us
  other arithmetic: 134 us -> 43.5 us
    all_to_all x3 -> x0, waiting for transfers between devices: 647 us -> none  [the longest x1 339 us: body(): lax.all_to_all(buffers, 'seq', split_axis=1, concat_axis=0, tiled=True)]
    all_to_all x1 -> x0, blocking collectives: 339 us -> none  [body(): lax.all_to_all(grad_expert, 'seq', split_axis=1, concat_axis=0, tiled=True)]
    dot_general x29 -> x9, matrix products: 322 us -> 58.4 us  [the longest x3 22.3 us: nt(): lax.dot_general(a, b, (((1,), (1,)), ((), ())), preferred_element_type=F32)]
    pallas_call x0 -> x6, Pallas kernels: none -> 257 us  [the longest x2 152 us: experts_pass(): pl.pallas_call(experts_kernel, grid=(experts,), in_specs=[fixed((tokens,...]
    all_gather x1 -> x2, blocking collectives: 399 us -> 169 us  [the longest x1 98.5 us: body(): lax.all_gather(w_router.astype(BF), everyone, axis=0, tiled=True)]
    ppermute x0 -> x8, waiting for transfers between devices: none -> 230 us  [swap(): return lax.ppermute(values, 'seq', [(i, i ^ bit) for i in range(n_seq)])]
    gather x2 -> x0, local copies, waits for them, and re-layouts: 182 us -> none  [take_rows(): return source[slot_row]]
    reduce_scatter x6 -> x5, waiting for transfers between devices: 439 us -> 568 us  [the longest x2 227 us: body(): lax.psum_scatter(g, 'dp', scatter_dimension=0).astype(F32)]
  transfers between devices with their start and end apart: 16 -> 19, of which waited for: 11 -> 10; matrix products, arithmetic and copies ran while one was open for 11% -> 8% of each run, Pallas kernels for 0% -> 8%
where the time goes in v1:
time: 1540 us; the launch traced here: 1530 us
  waiting for transfers between devices  905 us (59%)
  Pallas kernels  257 us (17%)
  blocking collectives  169 us (11%)
  local copies, waits for them, and re-layouts  75.2 us (5%)
  matrix products  58.4 us (4%)
  other arithmetic  43.5 us (3%)
    ppermute x8, waiting for transfers between devices, swap(): return lax.ppermute(values, 'seq', [(i, i ^ bit) for i in range(n_seq)])  230 us
    reduce_scatter x2, waiting for transfers between devices, body(): lax.psum_scatter(g, 'dp', scatter_dimension=0).astype(F32)  227 us
    reduce_scatter x1, waiting for transfers between devices, body(): lax.psum_scatter(grad_out, everyone, scatter_dimension=0, tiled=True)  152 us
    pallas_call x2, Pallas kernels, experts_pass(): pl.pallas_call(experts_kernel, grid=(experts,), in_specs=[fixed((tokens,...  152 us
    reduce_scatter x1, waiting for transfers between devices, body(): lax.psum_scatter(grad_qkv, everyone, scatter_dimension=0, tiled=True)  124 us
    all_gather x1, blocking collectives, body(): lax.all_gather(w_router.astype(BF), everyone, axis=0, tiled=True)  98.5 us
    unnamed x12, waiting for transfers between devices  91.4 us
    all_gather x1, blocking collectives, body(): lax.all_gather(jnp.stack([attn_gain, ffn_gain]).astype(BF), everyone, axi...  70.3 us
  transfers between devices with their start and end apart: 19, of which 10 were waited for; matrix products, arithmetic and copies ran while one was open for 8% of the time, Pallas kernels for 8%

profile of v1, /device:TPU:0, one launch (start us, length us, event | category | flops | bytes accessed | tf_op | source)
XLA Modules:
  0.0 1531.1 jit_solution(8399143546113335935)
XLA Ops:
  9.9 70.3 %all-gather.3 = bf16[32,48,2]{1,2,0:T(2,128)(2,1)S(1)} all-gather(bf16[1,48,2]{1,2,0:T(2,128)(2,1)S(1)} %maximum_bitcast_fusion), channel_id=1, replica_groups=mesh['dp'=8,'seq'=4] {'dp','seq'}, dimensions={0}, use_global_device_ids=true | all-gather | bytes 6336 | tf_op jit(solution)/shard_map/all_gather | solution.py:458
  83.5 5.8 all-gather.11.cloned.1.call-done
  89.3 9.4 fusion.x_ref
  98.7 5.1 rope.1
  109.8 171.7 %collective-permute-done.3 = bf16[4,192,1536]{2,1,0:T(8,128)(2,1)S(1)} collective-permute-done((bf16[4,192,1536]{2,1,0:T(8,128)(2,1)}, bf16[4,192,1536]{2,1,0:T(8,128)(2,1)S(1)}, u32[]{:S(2)}, u32[]{:S(2)}) %collective-permute-start.3) | collective-permute-done | bytes 2359328 | tf_op jit(solution)/shard_map/ppermute | solution.py:456
  289.0 39.4 %attention.1 = (bf16[2,256,1536]{2,1,0:T(8,128)(2,1)}, f32[2,4,256,128]{3,2,1,0:T(8,128)}) custom-call(s32[3]{0:T(128)} %pad_add_fusion.1.info_ref, bf16[2,256,1536]{2,1,0:T(8,128)(2,1)} %get-tuple-element.23.q_ref, bf16[4,2,2,256,512]{4,3,2,1,0:T(8,128)(2,1)} %bitcast.69, bf16[4,2,2,256,512]{4,3,2,1,0:T(8,128)(2,1)} %bitcast.70), custom_call_target="tpu_custom_call" | custom-call | tf_op jit(solution)/shard_map/attention/pallas_call | solution.py:204
  328.5 10.6 all-gather.13.cloned.1.call-done
  339.1 6.8 multiply_reduce_fusion.4
  352.1 98.5 %all-gather.4 = bf16[32,48,16]{1,2,0:T(8,128)(2,1)S(1)} all-gather(bf16[1,48,16]{1,2,0:T(8,128)(2,1)S(1)} %convert_bitcast_fusion.3), channel_id=1, replica_groups=mesh['dp'=8,'seq'=4] {'dp','seq'}, dimensions={0}, use_global_device_ids=true | all-gather | bytes 50688 | tf_op jit(solution)/shard_map/all_gather | solution.py:464
  451.2 5.2 fusion.17
  456.3 4.7 copy.126.go_ref
  461.0 4.3 fusion.18
  474.9 76.0 %experts.2 = (bf16[1024,1536]{1,0:T(8,128)(2,1)}, bf16[1024,1536]{1,0:T(8,128)(2,1)}, f32[1024,128]{1,0:T(8,128)}, bf16[8,4,192,1536]{3,2,1,0:T(8,128)(2,1)}) custom-call(bf16[1024,1536]{1,0:T(8,128)(2,1)} %copy.125.h_ref, bf16[1536,1024]{1,0:T(8,128)(2,1)} %get-tuple-element.93.ht_ref, bf16[1024,1536]{1,0:T(8,128)(2,1)} %copy.126.go_ref, ...), custom_call_target="tpu_custom_call" | custom-call | flops 57982058496 | bytes 37748736 | tf_op jit(solution)/shard_map/experts/pallas_call | solution.py:402
  550.9 4.8 copy.127
  560.4 76.3 %experts.3 = (bf16[1024,1536]{1,0:T(8,128)(2,1)}, bf16[1024,1536]{1,0:T(8,128)(2,1)}, f32[1024,128]{1,0:T(8,128)}, bf16[8,4,192,1536]{3,2,1,0:T(8,128)(2,1)}) custom-call(bf16[1024,1536]{1,0:T(8,128)(2,1)} %copy.125.h_ref, bf16[1536,1024]{1,0:T(8,128)(2,1)} %get-tuple-element.93.ht_ref, bf16[1024,1536]{1,0:T(8,128)(2,1)} %copy.126.go_ref, ...), custom_call_target="tpu_custom_call" | custom-call | flops 57982058496 | bytes 37748736 | tf_op jit(solution)/shard_map/experts/pallas_call | solution.py:402
  636.6 4.7 copy.130
  641.3 4.8 copy.132
  664.9 57.9 %collective-permute-done.6 = f32[512,8]{1,0:T(8,128)} collective-permute-done((f32[512,8]{1,0:T(8,128)}, f32[512,8]{1,0:T(8,128)}, u32[]{:S(2)}, u32[]{:S(2)}) %collective-permute-start.6) | collective-permute-done | bytes 16416 | tf_op jit(solution)/shard_map/ppermute | solution.py:456
  731.7 3.8 multiply_reduce_fusion
  739.2 4.3 fusion.7
  743.5 54.7 %attention_back.1 = (f32[2,256,1536]{2,1,0:T(8,128)}, bf16[4,2,2,256,512]{4,3,2,1,0:T(8,128)(2,1)}) custom-call(s32[3]{0:T(128)} %pad_add_fusion.1.info_ref, bf16[2,256,1536]{2,1,0:T(8,128)(2,1)} %get-tuple-element.23.q_ref, bf16[4,2,2,256,512]{4,3,2,1,0:T(8,128)(2,1)} %bitcast.71, bf16[4,2,2,256,512]{4,3,2,1,0:T(8,128)(2,1)} %bitcast.72, ...), custom_call_target="tpu_custom_call" | custom-call | tf_op jit(solution)/shard_map/attention_back/pallas_call | solution.py:286
  800.3 5.6 convolution_convert_fusion
  808.4 64.2 %reduce-scatter.9.cloned.1.call-done = bf16[1,2,2,256,512]{4,3,2,1,0:T(8,128)(2,1)} async-done(((bf16[4,2,2,256,512]{4,3,2,1,0:T(8,128)(2,1)}), bf16[1,2,2,256,512]{4,3,2,1,0:T(8,128)(2,1)}) %reduce-scatter.9.cloned.1.call-update) | async-done | bytes 1048592 | tf_op jit(solution)/shard_map/reduce_scatter | solution.py:537
  872.7 5.0 unrope.1
  877.7 11.7 multiply_reduce_fusion.1
  890.8 11.8 bitcast_convert_fusion
  903.4 99.9 %reduce-scatter.17.cloned.1.call-done = bf16[1,4,192,1536]{3,2,1,0:T(8,128)(2,1)} async-done(((bf16[8,4,192,1536]{3,2,1,0:T(8,128)(2,1)}), bf16[1,4,192,1536]{3,2,1,0:T(8,128)(2,1)}) %reduce-scatter.17.cloned.1.call-update) | async-done | bytes 2359312 | tf_op jit(solution)/shard_map/reduce_scatter | solution.py:544
  1008.3 152.4 %reduce-scatter.13.cloned.1.call-done = bf16[48,1536]{1,0:T(8,128)(2,1)} async-done(((bf16[1536,1536]{1,0:T(8,128)(2,1)}), bf16[48,1536]{1,0:T(8,128)(2,1)}) %reduce-scatter.13.cloned.1.call-update) | async-done | bytes 147472 | tf_op jit(solution)/shard_map/reduce_scatter | solution.py:551
  1162.4 5.2 multiply_add_fusion
  1171.1 89.9 %reduce-scatter.19.cloned.1.call-done = f32[48,18]{1,0:T(8,128)} async-done(((f32[1536,18]{1,0:T(8,128)}), f32[48,18]{1,0:T(8,128)}) %reduce-scatter.19.cloned.1.call-update) | async-done | bytes 3472
  1264.5 124.3 %reduce-scatter.11.cloned.1.call-done = bf16[48,2560]{1,0:T(8,128)(2,1)} async-done(((bf16[1536,2560]{1,0:T(8,128)(2,1)}), bf16[48,2560]{1,0:T(8,128)(2,1)}) %reduce-scatter.11.cloned.1.call-update) | async-done | bytes 245776 | tf_op jit(solution)/shard_map/reduce_scatter | solution.py:552
  1390.6 127.3 %reduce-scatter.15.cloned.1.call-done = bf16[1,4,192,1536]{3,2,1,0:T(8,128)(2,1)} async-done(((bf16[8,4,192,1536]{3,2,1,0:T(8,128)(2,1)}), bf16[1,4,192,1536]{3,2,1,0:T(8,128)(2,1)}) %reduce-scatter.15.cloned.1.call-update) | async-done | bytes 2359312 | tf_op jit(solution)/shard_map/reduce_scatter | solution.py:544
  (187 shorter events, 99.8 us)
Async XLA Ops:
  7.2 75.4 %copy-start.12 = (bf16[2,256,1536]{2,1,0:T(8,128)(2,1)S(1)}, bf16[2,256,1536]{2,1,0:T(8,128)(2,1)}, u32[]{:S(2)}) copy-start(bf16[2,256,1536]{2,1,0:T(8,128)(2,1)} %param.11) | copy-start | bytes 4718596
  7.2 82.1 %all-gather.11.cloned.1.call-start = ((), (), s32[]{:S(2)}) async-start(), calls=%async_computation.6 | async-start | bytes 8110080 | tf_op jit(solution)/shard_map/all_gather | solution.py:460
  9.1 279.9 %all-gather.15.cloned.1.call-start = ((), (), s32[]{:S(2)}) async-start(), calls=%async_computation.13 | async-start | bytes 5242880 | tf_op jit(solution)/shard_map/all_gather | solution.py:480
  81.7 7.5 copy-start.24
  81.7 264.2 %copy-start.20 = (f32[1536]{0:T(1024)}, f32[1536]{0:T(1024)S(1)}, u32[]{:S(2)}) copy-start(f32[1536]{0:T(1024)S(1)} %get-tuple-element.86) | copy-start | bytes 18436
  103.8 235.3 %all-gather.13.cloned.1.call-start = ((), (), s32[]{:S(2)}) async-start(), calls=%async_computation.7 | async-start | bytes 4866048 | tf_op jit(solution)/shard_map/all_gather | solution.py:463
  104.6 370.4 %all-gather.17.cloned.1.call-start = ((), (), s32[]{:S(2)}) async-start(), calls=%async_computation.14 | async-start | bytes 21233664 | tf_op jit(solution)/shard_map/all_gather | solution.py:465
  107.8 452.6 %all-gather.19.cloned.1.call-start = ((), (), s32[]{:S(2)}) async-start(), calls=%async_computation.15 | async-start | bytes 21233664 | tf_op jit(solution)/shard_map/all_gather | solution.py:465
  107.9 173.6 %collective-permute-start.3 = (bf16[4,192,1536]{2,1,0:T(8,128)(2,1)}, bf16[4,192,1536]{2,1,0:T(8,128)(2,1)S(1)}, u32[]{:S(2)}, u32[]{:S(2)}) collective-permute-start(bf16[4,192,1536]{2,1,0:T(8,128)(2,1)} %pad_maximum_fusion.2), channel_id=1, source_target_pairs={{0,2},{1,3},{2,0},{3,1},{4,6},{5,7},{6,4},{7,5},{8,10},{9,11},{10,... | collective-permute-start | bytes 7077896 | tf_op jit(solution)/shard_map/ppermute | solution.py:456
  283.0 589.7 %reduce-scatter.9.cloned.1.call-start = ((), (), s32[]{:S(2)}) async-start(), calls=%async_computation.8 | async-start | bytes 5242880 | tf_op jit(solution)/shard_map/reduce_scatter | solution.py:537
  284.8 166.4 %copy-start.6 = (bf16[512,1536]{0,1:T(8,128)(2,1)}, bf16[512,1536]{0,1:T(8,128)(2,1)S(1)}, u32[]{:S(2)}) copy-start(bf16[512,1536]{0,1:T(8,128)(2,1)S(1)} %copy.146) | copy-start | bytes 4718596
  284.8 166.4 %collective-permute-start.1 = (bf16[512,1536]{0,1:T(8,128)(2,1)S(1)}, bf16[512,1536]{0,1:T(8,128)(2,1)}, u32[]{:S(2)}, u32[]{:S(2)}) collective-permute-start(bf16[512,1536]{0,1:T(8,128)(2,1)S(1)} %copy.146), channel_id=1, source_target_pairs={{0,1},{1,0},{2,3},{3,2},{4,5},{5,4},{6,7},{7,6},{8,9},{9,8},{10,11... | collective-permute-start | bytes 4718600 | tf_op jit(solution)/shard_map/ppermute | solution.py:456
  345.8 6.2 copy-start.26
  345.8 6.3 copy-start.28
  345.9 105.0 %copy-start.22 = (f32[512]{0:T(512)}, f32[512]{0:T(512)S(1)}, u32[]{:S(2)}) copy-start(f32[512]{0:T(512)S(1)} %add_rsqrt_fusion) | copy-start | bytes 6148
  349.0 112.0 %collective-permute-start = (bf16[512,1536]{0,1:T(8,128)(2,1)}, bf16[512,1536]{0,1:T(8,128)(2,1)}, u32[]{:S(2)}, u32[]{:S(2)}) collective-permute-start(bf16[512,1536]{0,1:T(8,128)(2,1)} %multiply_convert_fusion.1), channel_id=1, source_target_pairs={{0,1},{1,0},{2,3},{3,2},{4,5},{5,4},{6,7},{7,6},{8,9},{9,8},{10,11... | collective-permute-start | bytes 4718600 | tf_op jit(solution)/shard_map/ppermute | solution.py:456
  352.1 98.8 %collective-permute-start.2 = (s32[512,8]{0,1:T(8,128)S(1)}, s32[512,8]{0,1:T(8,128)S(1)}, u32[]{:S(2)}, u32[]{:S(2)}) collective-permute-start(s32[512,8]{0,1:T(8,128)S(1)} %bitcast.88), channel_id=1, source_target_pairs={{0,1},{1,0},{2,3},{3,2},{4,5},{5,4},{6,7},{7,6},{8,9},{9,8},{10,11... | collective-permute-start | bytes 49160 | tf_op jit(solution)/shard_map/ppermute | solution.py:456
  450.8 17.5 %copy-start.19 = (bf16[1536,16]{0,1:T(8,128)(2,1)}, bf16[1536,16]{0,1:T(8,128)(2,1)S(1)}, u32[]{:S(2)}) copy-start(bf16[1536,16]{0,1:T(8,128)(2,1)S(1)} %reshape.163) | copy-start | bytes 147460
  651.0 80.6 %collective-permute-start.5 = (bf16[512,1536]{0,1:T(8,128)(2,1)}, bf16[512,1536]{0,1:T(8,128)(2,1)}, u32[]{:S(2)}, u32[]{:S(2)}) collective-permute-start(bf16[512,1536]{0,1:T(8,128)(2,1)} %slice.109), channel_id=1, source_target_pairs={{0,1},{1,0},{2,3},{3,2},{4,5},{5,4},{6,7},{7,6},{8,9},{9,8},{10,11... | collective-permute-start | bytes 4718600 | tf_op jit(solution)/shard_map/ppermute | solution.py:456
  656.7 78.7 %collective-permute-start.4 = (bf16[512,1536]{0,1:T(8,128)(2,1)}, bf16[512,1536]{0,1:T(8,128)(2,1)}, u32[]{:S(2)}, u32[]{:S(2)}) collective-permute-start(bf16[512,1536]{0,1:T(8,128)(2,1)} %slice.110), channel_id=1, source_target_pairs={{0,1},{1,0},{2,3},{3,2},{4,5},{5,4},{6,7},{7,6},{8,9},{9,8},{10,11... | collective-permute-start | bytes 4718600 | tf_op jit(solution)/shard_map/ppermute | solution.py:456
  658.4 73.2 %copy-start.3 = (f32[512,1536]{0,1:T(8,128)S(1)}, f32[512,1536]{0,1:T(8,128)}, u32[]{:S(2)}) copy-start(f32[512,1536]{0,1:T(8,128)} %copy-done.2) | copy-start | bytes 9437188
  658.4 73.2 %copy-start.21 = (f32[1536]{0:T(1024)S(1)}, f32[1536]{0:T(1024)}, u32[]{:S(2)}) copy-start(f32[1536]{0:T(1024)} %copy-done.20) | copy-start | bytes 18436
  658.4 73.2 %copy-start.23 = (f32[512]{0:T(512)S(1)}, f32[512]{0:T(512)}, u32[]{:S(2)}) copy-start(f32[512]{0:T(512)} %copy-done.22) | copy-start | bytes 6148
  660.0 62.8 %collective-permute-start.6 = (f32[512,8]{1,0:T(8,128)}, f32[512,8]{1,0:T(8,128)}, u32[]{:S(2)}, u32[]{:S(2)}) collective-permute-start(f32[512,8]{1,0:T(8,128)} %pad_maximum_fusion.3), channel_id=1, source_target_pairs={{0,1},{1,0},{2,3},{3,2},{4,5},{5,4},{6,7},{7,6},{8,9},{9,8},{10,11... | collective-permute-start | bytes 49160 | tf_op jit(solution)/shard_map/ppermute | solution.py:456
  731.6 7.6 slice-start.2
  798.3 205.0 %reduce-scatter.17.cloned.1.call-start = ((), (), s32[]{:S(2)}) async-start(), calls=%async_computation.12 | async-start | bytes 21233664 | tf_op jit(solution)/shard_map/reduce_scatter | solution.py:544
  799.1 361.6 %reduce-scatter.13.cloned.1.call-start = ((), (), s32[]{:S(2)}) async-start(), calls=%async_computation.10 | async-start | bytes 4866048 | tf_op jit(solution)/shard_map/reduce_scatter | solution.py:551
  805.9 455.1 %reduce-scatter.19.cloned.1.call-start = ((), (), s32[]{:S(2)}) async-start(), calls=%async_computation.16 | async-start | bytes 811008
  877.7 13.1 copy-start.30
  890.7 498.1 %reduce-scatter.11.cloned.1.call-start = ((), (), s32[]{:S(2)}) async-start(), calls=%async_computation.9 | async-start | bytes 8110080 | tf_op jit(solution)/shard_map/reduce_scatter | solution.py:552
  902.7 615.1 %reduce-scatter.15.cloned.1.call-start = ((), (), s32[]{:S(2)}) async-start(), calls=%async_computation.11 | async-start | bytes 21233664 | tf_op jit(solution)/shard_map/reduce_scatter | solution.py:544
  1003.3 514.5 %collective-permute-start.7 = (bf16[4,192,1536]{2,1,0:T(8,128)(2,1)}, bf16[4,192,1536]{2,1,0:T(8,128)(2,1)}, u32[]{:S(2)}, u32[]{:S(2)}) collective-permute-start(bf16[4,192,1536]{2,1,0:T(8,128)(2,1)} %bitcast.96), channel_id=1, source_target_pairs={{0,2},{1,3},{2,0},{3,1},{4,6},{5,7},{6,4},{7,5},{8,10},{9,11},{10,... | collective-permute-start | bytes 7077896 | tf_op jit(solution)/shard_map/ppermute | solution.py:456
  (23 other events, 85.1 us)
Sparse Core Ops, SparseCore 0:
  11.4 77.8 all-gather.10
  103.9 160.9 all-gather.14
  268.3 70.7 all-gather.12
  340.8 99.2 all-gather.16
  441.8 98.5 all-gather.18
  798.4 74.2 reduce-scatter.8
  876.3 126.9 reduce-scatter.16
  1008.8 151.9 reduce-scatter.12
  1165.8 95.1 reduce-scatter.18
  1266.5 122.2 reduce-scatter.10
  1392.4 125.3 reduce-scatter.14
